TPU v7x, 32 devices: a whole 2x2x4 slice. The times are simulated.
32 devices in a mesh: row: 8 (over z, core), col: 4 (over y, x).
Axes of the slice: x: 2, y: 2, z: 4, core: 2. Of those that a mesh axis runs over, the one named last changes fastest.
Arguments:
- u_start: float32 [128, 131072], P('col', 'row'), may hold values from -24 to 24
- v_start: float32 [128, 65536], P('row', 'col'), may hold values from -24 to 24
- keep_u: float32 [128, 40], replicated, may hold values from -1 to 1, as said below
- keep_v: float32 [128, 40], replicated, may hold values from -1 to 1, as said below
- v_next: float32 [65536], P(('col', 'row')), may hold values from -96 to 96
- tile_blocks: bfloat16 [2048, 256, 256], P(('row', 'col')), may hold values from -0.375 to 0.375
- tile_rows: int32 [2048], P(('row', 'col')), may hold values from 0 to 63
- tile_cols: int32 [2048], P(('row', 'col')), may hold values from 0 to 63
- tile_count: int32 [32], P(('row', 'col')), may hold values from 32 to 64
Outputs:
- u_basis: float32 [42, 131072], P(None, ('row', 'col'))
- v_basis: float32 [43, 65536], P(None, ('col', 'row'))
- bidiagonal: float32 [2, 2], replicated
Inputs may be any that keep to these rules, and one draw needn't show every extreme that they name: `tile_rows`: tile row within the device's row group. `tile_cols`: tile column within the device's column group. `tile_count`: slots at this index and beyond hold no tile. `keep_u`: the columns are orthonormal. `keep_v`: the columns are orthonormal.
All inputs are finite; a program needn't handle non-finite values.
Results may differ from a plain program's by a relative error of at most 0.00155.
Values may be sent and summed in bfloat16 or wider, within the bound.
A program may use at most 64 MiB of HBM per device.

v0:
```python
import functools

import jax
import jax.numpy as jnp
from jax import lax
from jax.experimental import pallas as pl
from jax.experimental.pallas import tpu as pltpu
from jax.sharding import PartitionSpec as P

STEPS = 2
HIGH = lax.Precision.HIGHEST
F32 = jnp.float32
BF16 = jnp.bfloat16
LANE = 128
HALF = 64
DIRECT = 32


def kernel(
    row_n, col_n, keep_n, u_hbm, v_hbm, keep_u, keep_v, v_next, tiles_hbm, rows_ref, cols_ref, count_ref,
    u_out, v_out, bi_out,
    u_all, v_all, tiles, u_rows, v_rows, u_vec, v_vec, big_col, big_row, sum_col, sum_row, sum_all,
    v_gather, u_gather, u_parts, v_parts, u_recv, v_recv, picked, products,
    local_sem, init_u_send, init_u_recv, init_v_send, init_v_recv, send_sem,
    sum_col_sem, sum_row_sem, sum_all_sem, big_col_send, big_col_sem, big_row_send, big_row_sem,
    vg_sem, ug_sem, ur_sem, vr_sem,
):
    row_me = lax.axis_index("row")
    col_me = lax.axis_index("col")
    barrier = pltpu.get_barrier_semaphore()
    direct = row_n * col_n <= DIRECT
    peers = [(a, b) for a in range(row_n) for b in range(col_n)
             if (a or b) and (direct or not (a and b))]
    for a, b in peers:
        where = {"row": lax.rem(row_me + a, row_n), "col": lax.rem(col_me + b, col_n)}
        pl.semaphore_signal(barrier, inc=1, device_id=where, device_id_type=pl.DeviceIdType.MESH)

    u_here, v_here = u_hbm.shape[0], v_hbm.shape[0]
    u_len, v_len = u_rows.shape[1], v_rows.shape[1]
    u_total = float(u_len * row_n * col_n)
    v_total = float(v_len * row_n * col_n)
    rows_p = u_rows.shape[0]
    keep_p = keep_u.shape[0]
    tile = tiles.shape[1]
    slots = tiles.shape[0]
    u_sub, v_sub = u_len // tile, v_len // tile

    def u_src(p):
        return u_hbm.at[:, pl.ds(pl.multiple_of(p * u_len, LANE), u_len)]

    def v_src(p):
        return v_hbm.at[:, pl.ds(pl.multiple_of(p * v_len, LANE), v_len)]

    u_dst = u_all.at[pl.ds(pl.multiple_of(col_me * u_here, 8), u_here), :]
    v_dst = v_all.at[pl.ds(pl.multiple_of(row_me * v_here, 8), v_here), :]
    own_v = pltpu.make_async_copy(v_src(row_me), v_dst, local_sem.at[0])
    own_u = pltpu.make_async_copy(u_src(col_me), u_dst, local_sem.at[1])
    own_t = pltpu.make_async_copy(tiles_hbm, tiles, local_sem.at[2])
    own_v.start()
    own_u.start()
    own_t.start()

    def send(axis, me, n, src, dst, sends, recvs):
        copies = []
        for k in range(1, n):
            target = lax.rem(me + k, n)
            copy = pltpu.make_async_remote_copy(
                src_ref=src(target, k), dst_ref=dst(k), send_sem=sends.at[k], recv_sem=recvs(k),
                device_id={axis: target}, device_id_type=pl.DeviceIdType.MESH)
            copy.start()
            copies.append(copy)
        return copies

    pl.semaphore_wait(barrier, len(peers))
    v_init = send("row", row_me, row_n, lambda p, k: v_src(p), lambda k: v_dst, init_v_send,
                  lambda k: init_v_recv.at[k])
    u_init = send("col", col_me, col_n, lambda p, k: u_src(p), lambda k: u_dst, init_u_send,
                  lambda k: init_u_recv.at[k])

    active = lax.broadcasted_iota(jnp.int32, (1, slots), 1) < count_ref[...]
    row_blocks = u_parts.shape[0] * u_sub
    col_blocks = v_parts.shape[0] * v_sub
    row_hot = jnp.where(
        (lax.broadcasted_iota(jnp.int32, (row_blocks, slots), 0) == rows_ref[...]) & active, 1.0, 0.0)
    col_hot = jnp.where(
        (lax.broadcasted_iota(jnp.int32, (col_blocks, slots), 0) == cols_ref[...]) & active, 1.0, 0.0)

    eye = (lax.broadcasted_iota(jnp.int32, (rows_p, LANE), 0)
           == lax.broadcasted_iota(jnp.int32, (rows_p, LANE), 1))
    row_id = lax.broadcasted_iota(jnp.int32, (rows_p, LANE), 0)
    lane_id = lax.broadcasted_iota(jnp.int32, (rows_p, LANE), 1)
    lane_row = lax.broadcasted_iota(jnp.int32, (1, LANE), 1)

    def to_row(column):
        return jnp.sum(jnp.where(eye, column, 0.0), axis=0, keepdims=True)

    def to_column(row):
        return jnp.sum(jnp.where(eye, row, 0.0), axis=1, keepdims=True)

    def add_up(buf, n):
        parts = [buf[i] for i in range(n)]
        while len(parts) > 1:
            parts = [parts[i] + parts[i + 1] if i + 1 < len(parts) else parts[i]
                     for i in range(0, len(parts), 2)]
        return parts[0]

    def col_start(buf, value, sends, recvs):
        buf[col_me] = value
        return send("col", col_me, col_n, lambda p, k: buf.at[col_me], lambda k: buf.at[col_me],
                    sends, recvs)

    def row_start(buf, value, sends, recvs):
        buf[row_me] = value
        return send("row", row_me, row_n, lambda p, k: buf.at[row_me], lambda k: buf.at[row_me],
                    sends, recvs)

    def sum_start(row, index):
        if not direct:
            return col_start(sum_col.at[index], row, send_sem, lambda k: sum_col_sem.at[index, k])
        me = row_me * col_n + col_me
        buf = sum_all.at[index]
        buf[me] = row
        copies = []
        for k, (a, b) in enumerate(peers):
            where = {"row": lax.rem(row_me + a, row_n), "col": lax.rem(col_me + b, col_n)}
            copy = pltpu.make_async_remote_copy(
                src_ref=buf.at[me], dst_ref=buf.at[me], send_sem=send_sem.at[k],
                recv_sem=sum_all_sem.at[index, k], device_id=where,
                device_id_type=pl.DeviceIdType.MESH)
            copy.start()
            copies.append(copy)
        return copies

    def sum_finish(copies, index):
        for copy in copies:
            copy.wait()
        if direct:
            return add_up(sum_all.at[index], row_n * col_n)
        buf = sum_row.at[index]
        for copy in row_start(buf, add_up(sum_col.at[index], col_n), send_sem,
                              lambda k: sum_row_sem.at[index, k]):
            copy.wait()
        return add_up(buf, row_n)

    def coef(basis, vec):
        acc = jnp.zeros((rows_p, LANE), F32)
        for j in range(vec.shape[1] // LANE):
            at = slice(j * LANE, (j + 1) * LANE)
            acc = acc + basis[:, at] * vec[:, at]
        return to_row(jnp.sum(acc, axis=1, keepdims=True))

    def remove(basis, vec, column):
        spread = jnp.broadcast_to(column, (rows_p, LANE))
        square = jnp.zeros((1, LANE), F32)
        for j in range(vec.shape[1] // LANE):
            at = slice(j * LANE, (j + 1) * LANE)
            new = vec[:, at] - jnp.sum(spread * basis[:, at], axis=0, keepdims=True)
            vec[:, at] = new
            square = square + new * new
        return jnp.sum(square, axis=1, keepdims=True)

    def orth(basis, vec, first_sum, index, length, gram_now, place, between=lambda: None):
        first = first_sum / length
        square = remove(basis, vec, to_column(first))
        copies = sum_start(coef(basis, vec) + jnp.where(lane_row == LANE - 1, square, 0.0), index)
        between()
        got = sum_finish(copies, index)
        square = jnp.sum(jnp.where(lane_row == LANE - 1, got, 0.0), axis=1, keepdims=True) / length
        second = jnp.where(lane_row < rows_p, got, 0.0) / length
        second_col = to_column(second)
        remove(basis, vec, second_col)
        gram = gram_now()
        gram_coef = jnp.sum(gram * second_col, axis=0, keepdims=True)
        square = (square - 2.0 * jnp.sum(second * second, axis=1, keepdims=True)
                  + jnp.sum(second * gram_coef, axis=1, keepdims=True))
        scale = jnp.sqrt(square + 1e-06)
        inverse = 1.0 / scale
        vec[...] = vec[...] * inverse

        def grow():
            basis[place:place + 1, :] = vec[...]
            cross = (second - gram_coef) * inverse
            grown = jnp.where(row_id == place, cross, gram)
            grown = jnp.where(lane_id == place, to_column(cross), grown)
            corner = (row_id == place) & (lane_id == place)
            return jnp.where(corner, square / (scale * scale), grown)

        return scale, grow

    def matvec(gathered, n, pick_hot, put_hot, contract):
        full = jnp.concatenate([gathered[i].astype(F32) for i in range(n)], axis=0).astype(BF16)
        picked[...] = lax.dot_general(pick_hot.astype(BF16), full, (((0,), (0,)), ((), ())),
                                      preferred_element_type=F32)
        sub = lax.broadcasted_iota(jnp.int32, (8, tile), 0)

        def group(g, carry):
            base = pl.multiple_of(g * 8, 8)
            left = picked[pl.ds(base, 8), :].astype(BF16)
            acc = jnp.zeros((8, tile), F32)
            for i in range(8):
                res = lax.dot_general(left, tiles[base + i], (((1,), (contract,)), ((), ())),
                                      preferred_element_type=F32)
                acc = jnp.where(sub == i, res, acc)
            products[pl.ds(base, 8), :] = acc
            return carry

        lax.fori_loop(0, slots // 8, group, 0)
        return jnp.dot(put_hot, products[...], precision=HIGH, preferred_element_type=F32)

    def gather(axis, me, n, vec, sub, buf, sems, grow):
        own = jnp.concatenate([vec[:, i * tile:(i + 1) * tile] for i in range(sub)], axis=0)
        buf[me] = own.astype(BF16)
        copies = send(axis, me, n, lambda p, k: buf.at[me], lambda k: buf.at[me], send_sem, sems)
        gram = grow()
        for copy in copies:
            copy.wait()
        return gram

    def scatter(axis, me, n, value, vec, sub, parts, recv, sems):
        for i in range(n):
            parts[i] = value[i * sub:(i + 1) * sub, :]
        for copy in send(axis, me, n, lambda p, k: parts.at[p], lambda k: recv.at[k], send_sem, sems):
            copy.wait()
        total = parts[me]
        for k in range(1, n):
            total = total + recv[k]
        for i in range(sub):
            vec[:, i * tile:(i + 1) * tile] = total[i:i + 1, :]

    u_rows[...] = jnp.zeros(u_rows.shape, F32)
    v_rows[...] = jnp.zeros(v_rows.shape, F32)
    v_vec[...] = v_next[...]
    own_v.wait()
    for copy in v_init:
        copy.wait()

    def kept(keep, source, target, length):
        for j in range(length // 512):
            at = slice(j * 512, (j + 1) * 512)
            target[0:keep_p, at] = jnp.dot(keep[...], source[:, at], precision=HIGH,
                                           preferred_element_type=F32)

    def half_gram(basis):
        small = basis[0:keep_p, :]
        wide = jnp.concatenate([basis[...], jnp.zeros((HALF - rows_p, basis.shape[1]), F32)], axis=0)
        return lax.dot_general(small, wide, (((1,), (1,)), ((), ())), precision=HIGH,
                               preferred_element_type=F32)

    kept(keep_v, v_all, v_rows, v_len)
    first_copies = sum_start(coef(v_rows, v_vec), 0)
    own_u.wait()
    for copy in u_init:
        copy.wait()
    kept(keep_u, u_all, u_rows, u_len)
    both = jnp.concatenate([half_gram(v_rows), half_gram(u_rows)], axis=1)
    gram_copies = col_start(big_col, both, big_col_send, lambda k: big_col_sem.at[k])

    def gram_step():
        for copy in gram_copies:
            copy.wait()
        gram_copies[:] = row_start(big_row, add_up(big_col, col_n), big_row_send,
                                   lambda k: big_row_sem.at[k])

    def gram_end():
        for copy in gram_copies:
            copy.wait()
        total = add_up(big_row, row_n)
        total = jnp.concatenate([total, jnp.zeros((rows_p - keep_p, LANE), F32)], axis=0)
        grams.append(jnp.where(lane_id < HALF, pltpu.roll(total, HALF, 1), 0.0) / u_total)
        return jnp.where(lane_id < HALF, total, 0.0) / v_total

    grams = []
    scale, grow = orth(v_rows, v_vec, sum_finish(first_copies, 0), 1, v_total, gram_end, keep_n,
                       gram_step)
    gram_u = grams[0]
    index = 2
    alphas, betas = [], []
    for step in range(STEPS):
        gram_v = gather("row", row_me, row_n, v_vec, v_sub, v_gather.at[step],
                        lambda k: vg_sem.at[step, k], grow)
        if step == 0:
            own_t.wait()
        partial = matvec(v_gather.at[step], row_n, col_hot, row_hot, 1)
        scatter("col", col_me, col_n, partial, u_vec, u_sub, u_parts, u_recv.at[step],
                lambda k: ur_sem.at[step, k])
        total = sum_finish(sum_start(coef(u_rows, u_vec), index), index)
        alpha, grow = orth(u_rows, u_vec, total, index + 1, u_total, lambda: gram_u, keep_n + step)
        gram_u = gather("col", col_me, col_n, u_vec, u_sub, u_gather.at[step],
                        lambda k: ug_sem.at[step, k], grow)
        partial = matvec(u_gather.at[step], col_n, row_hot, col_hot, 0)
        scatter("row", row_me, row_n, partial, v_vec, v_sub, v_parts, v_recv.at[step],
                lambda k: vr_sem.at[step, k])
        total = sum_finish(sum_start(coef(v_rows, v_vec), index + 2), index + 2)
        beta, grow = orth(v_rows, v_vec, total, index + 3, v_total, lambda: gram_v, keep_n + 1 + step)
        index += 4
        alphas.append(alpha)
        betas.append(beta)
    grow()
    place_r = lax.broadcasted_iota(jnp.int32, (8, LANE), 0)
    place_l = lax.broadcasted_iota(jnp.int32, (8, LANE), 1)
    result = jnp.zeros((8, LANE), F32)
    for step in range(STEPS):
        result = jnp.where((place_r == 0) & (place_l == step), alphas[step], result)
        result = jnp.where((place_r == 1) & (place_l == step), betas[step], result)
    bi_out[...] = result
    u_out[...] = u_rows[0:u_out.shape[0], :]
    v_out[...] = v_rows[0:v_out.shape[0], :]


def per_device(
    u_start, v_start, keep_u, keep_v, v_next, tile_blocks, tile_rows, tile_cols, tile_count
):
    row_n = lax.axis_size("row")
    col_n = lax.axis_size("col")
    u_here, v_here = u_start.shape[0], v_start.shape[0]
    basis, keep_n = keep_u.shape
    u_len = u_start.shape[1] // col_n
    v_len = v_start.shape[1] // row_n
    slots, tile = tile_blocks.shape[0], tile_blocks.shape[1]
    rows_p = -(-(keep_n + 1 + STEPS) // 8) * 8
    keep_p = -(-keep_n // 8) * 8
    assert rows_p <= HALF
    pad = ((0, keep_p - keep_n), (0, 0))
    sums = 2 + 4 * STEPS
    total_n = row_n * col_n
    direct_n = total_n if total_n <= DIRECT else 1
    staged = 1 if total_n <= DIRECT else sums
    dma = pltpu.SemaphoreType.DMA
    vmem = pl.BlockSpec(memory_space=pltpu.VMEM)
    hbm = pl.BlockSpec(memory_space=pl.ANY)
    u_sub, v_sub = u_len // tile, v_len // tile
    u_basis, v_basis, bidiagonal = pl.pallas_call(
        functools.partial(kernel, row_n, col_n, keep_n),
        out_shape=(
            jax.ShapeDtypeStruct((keep_n + STEPS, u_len), F32),
            jax.ShapeDtypeStruct((keep_n + 1 + STEPS, v_len), F32),
            jax.ShapeDtypeStruct((8, LANE), F32),
        ),
        in_specs=[hbm, hbm, vmem, vmem, vmem, hbm, vmem, vmem, vmem],
        out_specs=(vmem, vmem, vmem),
        scratch_shapes=[
            pltpu.VMEM((basis, u_len), F32),
            pltpu.VMEM((basis, v_len), F32),
            pltpu.VMEM(tile_blocks.shape, BF16),
            pltpu.VMEM((rows_p, u_len), F32),
            pltpu.VMEM((rows_p, v_len), F32),
            pltpu.VMEM((1, u_len), F32),
            pltpu.VMEM((1, v_len), F32),
            pltpu.VMEM((col_n, keep_p, LANE), F32),
            pltpu.VMEM((row_n, keep_p, LANE), F32),
            pltpu.VMEM((staged, col_n, 1, LANE), F32),
            pltpu.VMEM((staged, row_n, 1, LANE), F32),
            pltpu.VMEM((sums, direct_n, 1, LANE), F32),
            pltpu.VMEM((STEPS, row_n, v_sub, tile), BF16),
            pltpu.VMEM((STEPS, col_n, u_sub, tile), BF16),
            pltpu.VMEM((col_n, u_sub, tile), F32),
            pltpu.VMEM((row_n, v_sub, tile), F32),
            pltpu.VMEM((STEPS, col_n, u_sub, tile), F32),
            pltpu.VMEM((STEPS, row_n, v_sub, tile), F32),
            pltpu.VMEM((slots, tile), F32),
            pltpu.VMEM((slots, tile), F32),
            dma((3,)),
            dma((col_n,)),
            dma((col_n,)),
            dma((row_n,)),
            dma((row_n,)),
            dma((max(row_n, col_n, direct_n),)),
            dma((staged, col_n)),
            dma((staged, row_n)),
            dma((sums, direct_n)),
            dma((col_n,)),
            dma((col_n,)),
            dma((row_n,)),
            dma((row_n,)),
            dma((STEPS, row_n)),
            dma((STEPS, col_n)),
            dma((STEPS, col_n)),
            dma((STEPS, row_n)),
        ],
        compiler_params=pltpu.CompilerParams(
            collective_id=0, has_side_effects=True, vmem_limit_bytes=48 * 1024 * 1024
        ),
    )(
        u_start, v_start, jnp.pad(keep_u.T, pad), jnp.pad(keep_v.T, pad), v_next.reshape(1, -1), tile_blocks,
        tile_rows.reshape(1, -1), tile_cols.reshape(1, -1), tile_count.reshape(1, 1),
    )
    return u_basis, v_basis, bidiagonal[:2, :STEPS]


def solution(mesh):
    return jax.shard_map(
        per_device,
        mesh=mesh,
        in_specs=(
            P("col", "row"),
            P("row", "col"),
            P(),
            P(),
            P(("col", "row")),
            P(("row", "col"), None, None),
            P(("row", "col")),
            P(("row", "col")),
            P(("row", "col")),
        ),
        out_specs=(P(None, ("row", "col")), P(None, ("col", "row")), P()),
        check_vma=False,
    )
```

profile of v0, /device:TPU:0, one launch (start us, length us, event | category | flops | bytes accessed | tf_op | source)
XLA Modules:
  0.0 133.2 jit_solution(12603945513314967519)
XLA Ops:
  1.3 0.0 copy-start
  1.3 1.6 %copy-done = f32[32,16384]{1,0:T(8,128)S(1)} copy-done((f32[32,16384]{1,0:T(8,128)S(1)}, f32[32,16384]{1,0:T(8,128)}, u32[]{:S(2)}) %copy-start) | copy-done | bytes 2097176
  2.9 0.0 copy-start.1
  2.9 1.2 copy-done.1
  4.1 0.0 copy-start.2
  4.1 0.7 copy-done.2
  4.8 0.0 copy-start.3
  4.8 0.7 copy-done.3
  5.6 0.0 copy-start.4
  5.6 0.7 copy-done.4
  6.3 0.0 copy-start.5
  6.3 0.7 copy-done.5
  6.9 0.0 copy-start.6
  6.9 0.7 copy-done.6
  7.6 123.4 %shard_map.112 = (f32[42,4096]{1,0:T(8,128)S(1)}, f32[43,2048]{1,0:T(8,128)S(1)}, f32[8,128]{1,0:T(8,128)S(1)}) custom-call(f32[32,16384]{1,0:T(8,128)S(1)} %copy-done, f32[16,16384]{1,0:T(8,128)S(1)} %copy-done.1, f32[40,128]{1,0:T(8,128)S(1)} %bitcast.7, f32[40,128]{1,0:T(8,128)S(1)} %bitcast.8, f32[1,2048]{1,0:T(1,128)S(1)} %bitcast.9, ...), custom_call_target="tpu_custom_call" | custom-call | tf_op jit(solution)/shard_map/pallas_call | solution.py:332
  131.0 0.6 slice.3
  131.6 0.9 copy.15
  132.4 0.7 copy.16
Async XLA Ops:
  1.3 1.6 %copy-start = (f32[32,16384]{1,0:T(8,128)S(1)}, f32[32,16384]{1,0:T(8,128)}, u32[]{:S(2)}) copy-start(f32[32,16384]{1,0:T(8,128)} %u_hbm.1) | copy-start | bytes 6291460
  2.9 1.2 copy-start.1
  4.1 0.7 copy-start.2
  4.8 0.7 copy-start.3
  5.6 0.7 copy-start.4
  6.3 0.7 copy-start.5
  6.9 0.7 copy-start.6
where the time goes:
time: 134 us; the launch traced here: 133 us
  Pallas kernels  123 us (92%)
  local copies, waits for them, and re-layouts  8.46 us (6%)
    pallas_call x1, Pallas kernels, per_device(): pl.pallas_call(functools.partial(kernel, row_n, col_n, keep_n), out_shape...  123 us
    unnamed x16, local copies, waits for them, and re-layouts  7.89 us

commit v1 on v0

v1 whole, which is shorter than its diff:
```python
import functools

import jax
import jax.numpy as jnp
from jax import lax
from jax.experimental import pallas as pl
from jax.experimental.pallas import tpu as pltpu
from jax.sharding import PartitionSpec as P

STEPS = 2
HIGH = lax.Precision.HIGHEST
F32 = jnp.float32
BF16 = jnp.bfloat16
I16 = jnp.int16
I32 = jnp.int32
LANE = 128
DIRECT = 32
KNEE = 5.0
FINE = 4800.0
COARSE = 461.0


def encode(x):
    code = x * COARSE + jnp.clip(x, -KNEE, KNEE) * (FINE - COARSE)
    return jnp.round(code).astype(I32).astype(I16)


def decode(code):
    y = code.astype(I32).astype(F32)
    near = jnp.clip(y, -KNEE * FINE, KNEE * FINE)
    return near * (1.0 / FINE) + (y - near) * (1.0 / COARSE)


def partner(me, k, n):
    if n & (n - 1):
        return lax.rem(me + k, n)
    other, bit = 0, 1
    while bit < n:
        digit = lax.rem(lax.div(me, bit), 2)
        other = other + (1 - digit if k & bit else digit) * bit
        bit *= 2
    return other


def kernel(
    row_n, col_n, keep_n, fold, u_hbm, v_hbm, keep_u_hbm, keep_v_hbm, v_next_hbm, tiles_hbm, rows_hbm, cols_hbm,
    count_hbm,
    u_out, v_out, bi_out,
    u_in, v_in, u_code, v_code, u_all, v_all, tiles, keep_u, keep_v, v_first, rows_ref, cols_ref, count_ref,
    u_rows, v_rows, u_vec, v_vec, gram_v_row, gram_v_col, gram_u_col, gram_u_row,
    sum_col, sum_row, sum_all, v_gather, u_gather, u_parts, v_parts, u_recv, v_recv,
    row_pick, col_pick, row_put, col_put, picked, products,
    local_sem, init_u_send, init_u_recv, init_v_send, init_v_recv, send_sem, gram_send, gram_recv,
    sum_col_sem, sum_row_sem, sum_all_sem, vg_sem, ug_sem, ur_sem, vr_sem,
):
    row_me = lax.axis_index("row")
    col_me = lax.axis_index("col")

    def load(index, source, target):
        copy = pltpu.make_async_copy(source, target, local_sem.at[index])
        copy.start()
        return copy

    own_v = load(0, v_hbm, v_in)
    own_u = load(1, u_hbm, u_in)
    own_keep_v = load(2, keep_v_hbm, keep_v)
    own_keep_u = load(3, keep_u_hbm, keep_u)
    own_next = load(4, v_next_hbm, v_first)
    own_places = [load(5, rows_hbm, rows_ref), load(6, cols_hbm, cols_ref), load(7, count_hbm, count_ref)]
    own_t = load(8, tiles_hbm, tiles)

    barrier = pltpu.get_barrier_semaphore()
    for k in range(1, row_n):
        pl.semaphore_signal(barrier, inc=1, device_id={"row": partner(row_me, k, row_n)},
                            device_id_type=pl.DeviceIdType.MESH)
    for k in range(1, col_n):
        pl.semaphore_signal(barrier, inc=1, device_id={"col": partner(col_me, k, col_n)},
                            device_id_type=pl.DeviceIdType.MESH)

    direct = row_n * col_n <= DIRECT
    v_here, u_here = v_all.shape[1], u_all.shape[1]
    u_len, v_len = u_rows.shape[1], v_rows.shape[1]
    u_total = float(u_len * row_n * col_n)
    v_total = float(v_len * row_n * col_n)
    rows_p = u_rows.shape[0]
    keep_p = keep_u.shape[0]
    tile = tiles.shape[1]
    slots = tiles.shape[0]
    u_sub, v_sub = u_len // tile, v_len // tile
    row_blocks, col_blocks = col_n * u_sub, row_n * v_sub
    width = LANE // fold
    part = rows_p // fold

    def send(axis, me, n, src, dst, sends, recvs):
        copies = []
        for k in range(n - 1, 0, -1):
            target = partner(me, k, n)
            copy = pltpu.make_async_remote_copy(
                src_ref=src(target), dst_ref=dst(k), send_sem=sends(k), recv_sem=recvs(k),
                device_id={axis: target}, device_id_type=pl.DeviceIdType.MESH)
            copy.start()
            copies.append(copy)
        return copies

    def finish(copies):
        for copy in copies:
            copy.wait()

    u_rows[...] = jnp.zeros(u_rows.shape, F32)
    v_rows[...] = jnp.zeros(v_rows.shape, F32)
    own_v.wait()
    for p in range(row_n):
        v_code[p] = encode(v_in[:, p * v_len:(p + 1) * v_len])
    own_u.wait()
    for p in range(col_n):
        u_code[p] = encode(u_in[:, p * u_len:(p + 1) * u_len])
    pl.semaphore_wait(barrier, row_n + col_n - 2)
    v_init = send("row", row_me, row_n, lambda p: v_code.at[p], lambda k: v_all.at[row_me],
                  lambda k: init_v_send.at[k], lambda k: init_v_recv.at[k])
    u_init = send("col", col_me, col_n, lambda p: u_code.at[p], lambda k: u_all.at[col_me],
                  lambda k: init_u_send.at[k], lambda k: init_u_recv.at[k])
    v_all[row_me] = v_code[row_me]
    u_all[col_me] = u_code[col_me]

    for copy in own_places:
        copy.wait()
    active = lax.broadcasted_iota(I32, (1, slots), 1) < count_ref[...]

    def hot_of(places, blocks, pick, put):
        hot = jnp.where(
            (lax.broadcasted_iota(I32, (blocks, slots), 0) == places) & active, 1.0, 0.0).astype(BF16)
        eye = (lax.broadcasted_iota(I32, (blocks, blocks), 0)
               == lax.broadcasted_iota(I32, (blocks, blocks), 1))
        pick[...] = lax.dot_general(hot, jnp.where(eye, 1.0, 0.0).astype(BF16), (((0,), (0,)), ((), ())),
                                    preferred_element_type=F32).astype(BF16)
        put[...] = jnp.concatenate([hot, hot, hot], axis=1)

    hot_of(rows_ref[...], row_blocks, row_pick, row_put)
    hot_of(cols_ref[...], col_blocks, col_pick, col_put)

    row_id = lax.broadcasted_iota(I32, (rows_p, LANE), 0)
    lane_id = lax.broadcasted_iota(I32, (rows_p, LANE), 1)
    lane_row = lax.broadcasted_iota(I32, (1, LANE), 1)
    eye = row_id == lane_id

    def to_row(column):
        return jnp.sum(jnp.where(eye, column, 0.0), axis=0, keepdims=True)

    def add_up(buf, n):
        parts = [buf[i] for i in range(n)]
        while len(parts) > 1:
            parts = [parts[i] + parts[i + 1] if i + 1 < len(parts) else parts[i]
                     for i in range(0, len(parts), 2)]
        return parts[0]

    def sum_all_devices(row, index):
        if direct:
            me = row_me * col_n + col_me
            buf = sum_all.at[index]
            buf[pl.ds(me, 1), :] = row
            pairs = [(a, b) for a in range(row_n) for b in range(col_n) if a or b]
            pairs.sort(key=lambda p: -(p[0] // 2 + bin(p[1]).count("1")))
            copies = []
            for k, (a, b) in enumerate(pairs):
                where = {"row": partner(row_me, a, row_n), "col": partner(col_me, b, col_n)}
                copy = pltpu.make_async_remote_copy(
                    src_ref=buf.at[pl.ds(me, 1)], dst_ref=buf.at[pl.ds(me, 1)], send_sem=send_sem.at[k],
                    recv_sem=sum_all_sem.at[index, k], device_id=where,
                    device_id_type=pl.DeviceIdType.MESH)
                copy.start()
                copies.append(copy)
            finish(copies)
            return jnp.sum(buf[...], axis=0, keepdims=True)
        buf = sum_col.at[index]
        buf[pl.ds(col_me, 1), :] = row
        finish(send("col", col_me, col_n, lambda p: buf.at[pl.ds(col_me, 1)], lambda k: buf.at[pl.ds(col_me, 1)],
                    lambda k: send_sem.at[k], lambda k: sum_col_sem.at[index, k]))
        row = jnp.sum(buf[...], axis=0, keepdims=True)
        buf = sum_row.at[index]
        buf[pl.ds(row_me, 1), :] = row
        finish(send("row", row_me, row_n, lambda p: buf.at[pl.ds(row_me, 1)], lambda k: buf.at[pl.ds(row_me, 1)],
                    lambda k: send_sem.at[k], lambda k: sum_row_sem.at[index, k]))
        return jnp.sum(buf[...], axis=0, keepdims=True)

    def coef(basis, place):
        acc = jnp.zeros((rows_p, LANE), F32)
        for j in range(basis.shape[1] // LANE):
            at = slice(j * LANE, (j + 1) * LANE)
            acc = acc + basis[:, at] * basis[place:place + 1, at]
        return to_row(jnp.sum(acc, axis=1, keepdims=True))

    def tables(gram, place):
        small = lax.dot_general(gram, gram, (((1,), (1,)), ((), ())), precision=HIGH, preferred_element_type=F32)
        square = jnp.concatenate([small, jnp.zeros((rows_p, LANE - rows_p), F32)], axis=1)
        one = jnp.where(eye & (row_id < place), 1.0, 0.0)
        return 2.0 * one - gram, one - (2.0 * gram - square), one

    def orth(basis, vec, row, place, table):
        both, left, one = table
        got = jnp.where(lane_row < place, row, 0.0)
        square = jnp.sum(jnp.where(lane_row == place, row, 0.0), axis=1, keepdims=True)
        column = jnp.sum(both * got, axis=1, keepdims=True)
        after = jnp.sum(left * got, axis=1, keepdims=True)
        first = jnp.sum(one * got, axis=1, keepdims=True)
        square = square - jnp.sum(column * (first + after), axis=0, keepdims=True)
        scale = jnp.sqrt(square + 1e-06)
        inverse = 1.0 / scale
        spread = jnp.broadcast_to(jnp.where(row_id[:, 0:1] == place, 1.0, -column), (rows_p, LANE))
        for j in range(basis.shape[1] // LANE):
            at = slice(j * LANE, (j + 1) * LANE)
            s, h = j * LANE // tile, j * LANE % tile
            vec[s:s + 1, h:h + LANE] = jnp.sum(spread * basis[:, at], axis=0, keepdims=True)
        out = vec[...] * inverse

        def grow(gram):
            for s in range(vec.shape[0]):
                basis[place:place + 1, s * tile:(s + 1) * tile] = out[s:s + 1, :]
            if gram is None:
                return None
            cross = after * inverse
            grown = jnp.where(row_id == place, to_row(cross), gram)
            grown = jnp.where(lane_id == place, cross, grown)
            corner = (row_id == place) & (lane_id == place)
            return jnp.where(corner, square / (scale * scale), grown)

        return scale, out, grow

    def matvec(gathered, n, pick, put, contract):
        full = jnp.concatenate([gathered[i].astype(F32) for i in range(n)], axis=0).astype(BF16)
        picked[...] = jnp.dot(pick[...], full, preferred_element_type=F32)
        sub = lax.broadcasted_iota(I32, (8, tile), 0)
        for g in range(slots // 8):
            left = picked[g * 8:(g + 1) * 8, :].astype(BF16)
            acc = jnp.zeros((8, tile), F32)
            for i in range(8):
                res = lax.dot_general(left, tiles[g * 8 + i], (((1,), (contract,)), ((), ())),
                                      preferred_element_type=F32)
                acc = jnp.where(sub == i, res, acc)
            products[g * 8:(g + 1) * 8, :] = acc
        full = products[...]
        high = full.astype(BF16)
        rest = full - high.astype(F32)
        middle = rest.astype(BF16)
        low = (rest - middle.astype(F32)).astype(BF16)
        return jnp.dot(put[...], jnp.concatenate([high, middle, low], axis=0), preferred_element_type=F32)

    def gather(axis, me, n, own, buf, sems, between):
        buf[me] = own.astype(BF16)
        copies = send(axis, me, n, lambda p: buf.at[me], lambda k: buf.at[me], lambda k: send_sem.at[k], sems)
        between()
        finish(copies)

    def scatter(axis, me, n, value, basis, place, sub, parts, recv, sems):
        for i in range(n):
            parts[i] = value[i * sub:(i + 1) * sub, :]
        finish(send(axis, me, n, lambda p: parts.at[p], lambda k: recv.at[k], lambda k: send_sem.at[k], sems))
        total = parts[me]
        for k in range(1, n):
            total = total + recv[k]
        for s in range(sub):
            basis[place:place + 1, s * tile:(s + 1) * tile] = total[s:s + 1, :]

    def kept(keep, source, target):
        factor = keep[...]
        high = factor.astype(BF16)
        low = (factor - high.astype(F32)).astype(BF16)
        left = jnp.concatenate(
            [jnp.concatenate([high, high], axis=1), jnp.concatenate([low, jnp.zeros(low.shape, BF16)], axis=1)], axis=0)
        step = min(512, target.shape[1])
        for j in range(target.shape[1] // step):
            at = slice(j * step, (j + 1) * step)
            data = jnp.concatenate([decode(source[i, :, at]) for i in range(source.shape[0])], axis=0)
            top = data.astype(BF16)
            rest = (data - top.astype(F32)).astype(BF16)
            both = jnp.dot(left, jnp.concatenate([top, rest], axis=0), preferred_element_type=F32)
            target[0:keep_p, at] = both[0:keep_p] + both[keep_p:2 * keep_p]

    def half_gram(basis):
        wide = basis[...]
        small = lax.dot_general(wide, wide, (((1,), (1,)), ((), ())), precision=HIGH, preferred_element_type=F32)
        full = jnp.concatenate([small, jnp.zeros((rows_p, LANE - rows_p), F32)], axis=1)
        packed = full[0:part]
        for g in range(1, fold):
            packed = packed + pltpu.roll(full[g * part:(g + 1) * part], g * width, 1)
        return packed

    def unpack(packed):
        pieces = [packed] + [pltpu.roll(packed, LANE - g * width, 1) for g in range(1, fold)]
        return jnp.where(lane_id < width, jnp.concatenate(pieces, axis=0), 0.0)

    def row_spread(buf, value, index):
        buf[row_me] = value
        return send("row", row_me, row_n, lambda p: buf.at[row_me], lambda k: buf.at[row_me],
                    lambda k: gram_send.at[index, k], lambda k: gram_recv.at[index, k])

    def col_spread(buf, value, index):
        buf[col_me] = value
        return send("col", col_me, col_n, lambda p: buf.at[col_me], lambda k: buf.at[col_me],
                    lambda k: gram_send.at[index, k], lambda k: gram_recv.at[index, k])

    own_next.wait()
    own_keep_v.wait()
    own_keep_u.wait()
    v_rows[keep_n:keep_n + 1, :] = v_first[...]
    finish(v_init)
    kept(keep_v, v_all, v_rows)
    v_copies = row_spread(gram_v_row, half_gram(v_rows), 0)
    finish(u_init)
    kept(keep_u, u_all, u_rows)
    u_copies = col_spread(gram_u_col, half_gram(u_rows), 1)
    finish(v_copies)
    v_copies = col_spread(gram_v_col, add_up(gram_v_row, row_n), 2)
    finish(u_copies)
    u_copies = row_spread(gram_u_row, add_up(gram_u_col, col_n), 3)
    finish(v_copies)
    wide = unpack(add_up(gram_v_col, col_n)) / v_total
    first_row = wide[keep_n:keep_n + 1, :]
    gram_v = jnp.where((row_id < keep_n) & (lane_id < keep_n), wide, 0.0)
    scale, out, grow = orth(v_rows, v_vec, first_row, keep_n, tables(gram_v, keep_n))

    state = {"v": gram_v, "u": None}

    def between_v(place, grow, step):
        def run():
            state["v"] = grow(state["v"])
            state["v_table"] = tables(state["v"], place + 1)
            if step == 0:
                finish(u_copies)
                gram_u = unpack(add_up(gram_u_row, row_n)) / u_total
                state["u"] = jnp.where((row_id < keep_n) & (lane_id < keep_n), gram_u, 0.0)
                state["u_table"] = tables(state["u"], keep_n)
        return run

    def between_u(place, grow, step):
        def run():
            if step + 1 < STEPS:
                state["u"] = grow(state["u"])
                state["u_table"] = tables(state["u"], place + 1)
            else:
                grow(None)
        return run

    alphas, betas = [], []
    for step in range(STEPS):
        u_place, v_place = keep_n + step, keep_n + 1 + step
        gather("row", row_me, row_n, out, v_gather.at[step], lambda k: vg_sem.at[step, k],
               between_v(v_place - 1, grow, step))
        if step == 0:
            own_t.wait()
        partial = matvec(v_gather.at[step], row_n, col_pick, row_put, 1)
        scatter("col", col_me, col_n, partial, u_rows, u_place, u_sub, u_parts, u_recv.at[step],
                lambda k: ur_sem.at[step, k])
        row = sum_all_devices(coef(u_rows, u_place), 2 * step) / u_total
        alpha, out, grow = orth(u_rows, u_vec, row, u_place, state["u_table"])
        gather("col", col_me, col_n, out, u_gather.at[step], lambda k: ug_sem.at[step, k],
               between_u(u_place, grow, step))
        partial = matvec(u_gather.at[step], col_n, row_pick, col_put, 0)
        scatter("row", row_me, row_n, partial, v_rows, v_place, v_sub, v_parts, v_recv.at[step],
                lambda k: vr_sem.at[step, k])
        row = sum_all_devices(coef(v_rows, v_place), 2 * step + 1) / v_total
        beta, out, grow = orth(v_rows, v_vec, row, v_place, state["v_table"])
        alphas.append(alpha)
        betas.append(beta)
    grow(None)
    place_r = lax.broadcasted_iota(I32, (8, LANE), 0)
    place_l = lax.broadcasted_iota(I32, (8, LANE), 1)
    result = jnp.zeros((8, LANE), F32)
    for step in range(STEPS):
        result = jnp.where((place_r == 0) & (place_l == step), alphas[step], result)
        result = jnp.where((place_r == 1) & (place_l == step), betas[step], result)
    bi_out[...] = result
    u_out[...] = u_rows[0:u_out.shape[0], :]
    v_out[...] = v_rows[0:v_out.shape[0], :]


def per_device(
    u_start, v_start, keep_u, keep_v, v_next, tile_blocks, tile_rows, tile_cols, tile_count
):
    row_n = lax.axis_size("row")
    col_n = lax.axis_size("col")
    u_here, v_here = u_start.shape[0], v_start.shape[0]
    basis, keep_n = keep_u.shape
    u_len = u_start.shape[1] // col_n
    v_len = v_start.shape[1] // row_n
    slots, tile = tile_blocks.shape[0], tile_blocks.shape[1]
    fold = max(f for f in (1, 2, 3) if f * (keep_n + 1) <= LANE)
    rows_p = -(-(keep_n + 1 + STEPS) // (8 * fold)) * 8 * fold
    keep_p = -(-keep_n // 8) * 8
    assert rows_p <= LANE
    pad = ((0, keep_p - keep_n), (0, 0))
    sums = 2 * STEPS
    total_n = row_n * col_n
    direct_n = total_n if total_n <= DIRECT else 1
    staged = 1 if total_n <= DIRECT else sums
    part = rows_p // fold
    dma = pltpu.SemaphoreType.DMA
    vmem = pl.BlockSpec(memory_space=pltpu.VMEM)
    hbm = pl.BlockSpec(memory_space=pltpu.HBM)
    u_sub, v_sub = u_len // tile, v_len // tile
    row_blocks, col_blocks = col_n * u_sub, row_n * v_sub
    most = max(row_n, col_n)
    u_basis, v_basis, bidiagonal = pl.pallas_call(
        functools.partial(kernel, row_n, col_n, keep_n, fold),
        out_shape=(
            jax.ShapeDtypeStruct((keep_n + STEPS, u_len), F32),
            jax.ShapeDtypeStruct((keep_n + 1 + STEPS, v_len), F32),
            jax.ShapeDtypeStruct((8, LANE), F32),
        ),
        in_specs=[hbm] * 9,
        out_specs=(vmem, vmem, vmem),
        scratch_shapes=[
            pltpu.VMEM(u_start.shape, F32),
            pltpu.VMEM(v_start.shape, F32),
            pltpu.VMEM((col_n, u_here, u_len), I16),
            pltpu.VMEM((row_n, v_here, v_len), I16),
            pltpu.VMEM((col_n, u_here, u_len), I16),
            pltpu.VMEM((row_n, v_here, v_len), I16),
            pltpu.VMEM(tile_blocks.shape, BF16),
            pltpu.VMEM((keep_p, basis), F32),
            pltpu.VMEM((keep_p, basis), F32),
            pltpu.VMEM((1, v_len), F32),
            pltpu.VMEM((1, slots), I32),
            pltpu.VMEM((1, slots), I32),
            pltpu.VMEM((1, 1), I32),
            pltpu.VMEM((rows_p, u_len), F32),
            pltpu.VMEM((rows_p, v_len), F32),
            pltpu.VMEM((u_sub, tile), F32),
            pltpu.VMEM((v_sub, tile), F32),
            pltpu.VMEM((row_n, part, LANE), F32),
            pltpu.VMEM((col_n, part, LANE), F32),
            pltpu.VMEM((col_n, part, LANE), F32),
            pltpu.VMEM((row_n, part, LANE), F32),
            pltpu.VMEM((staged, col_n, LANE), F32),
            pltpu.VMEM((staged, row_n, LANE), F32),
            pltpu.VMEM((sums, direct_n, LANE), F32),
            pltpu.VMEM((STEPS, row_n, v_sub, tile), BF16),
            pltpu.VMEM((STEPS, col_n, u_sub, tile), BF16),
            pltpu.VMEM((col_n, u_sub, tile), F32),
            pltpu.VMEM((row_n, v_sub, tile), F32),
            pltpu.VMEM((STEPS, col_n, u_sub, tile), F32),
            pltpu.VMEM((STEPS, row_n, v_sub, tile), F32),
            pltpu.VMEM((slots, row_blocks), BF16),
            pltpu.VMEM((slots, col_blocks), BF16),
            pltpu.VMEM((row_blocks, 3 * slots), BF16),
            pltpu.VMEM((col_blocks, 3 * slots), BF16),
            pltpu.VMEM((slots, tile), F32),
            pltpu.VMEM((slots, tile), F32),
            dma((9,)),
            dma((col_n,)),
            dma((col_n,)),
            dma((row_n,)),
            dma((row_n,)),
            dma((max(most, direct_n),)),
            dma((4, most)),
            dma((4, most)),
            dma((staged, col_n)),
            dma((staged, row_n)),
            dma((sums, direct_n)),
            dma((STEPS, row_n)),
            dma((STEPS, col_n)),
            dma((STEPS, col_n)),
            dma((STEPS, row_n)),
        ],
        compiler_params=pltpu.CompilerParams(
            collective_id=0, has_side_effects=True, vmem_limit_bytes=62 * 1024 * 1024
        ),
    )(
        u_start, v_start, jnp.pad(keep_u.T, pad), jnp.pad(keep_v.T, pad), v_next.reshape(1, -1), tile_blocks,
        tile_rows.reshape(1, -1), tile_cols.reshape(1, -1), tile_count.reshape(1, 1),
    )
    return u_basis, v_basis, bidiagonal[:2, :STEPS]


def solution(mesh):
    return jax.shard_map(
        per_device,
        mesh=mesh,
        in_specs=(
            P("col", "row"),
            P("row", "col"),
            P(),
            P(),
            P(("col", "row")),
            P(("row", "col"), None, None),
            P(("row", "col")),
            P(("row", "col")),
            P(("row", "col")),
        ),
        out_specs=(P(None, ("row", "col")), P(None, ("col", "row")), P()),
        check_vma=False,
    )
```

time: 134 us -> 92.4 us (0.69)
  Pallas kernels: 123 us -> 85.8 us
  local copies, waits for them, and re-layouts: 8.46 us -> 5.07 us
    pallas_call x1, Pallas kernels: 123 us -> 85.8 us  [per_device(): pl.pallas_call(functools.partial(kernel, row_n, col_n, keep_n, fold), out...]
    unnamed x16 -> x2, local copies, waits for them, and re-layouts: 7.89 us -> 3.83 us
where the time goes in v1:
time: 92.4 us; the launch traced here: 92.2 us
  Pallas kernels  85.8 us (93%)
  local copies, waits for them, and re-layouts  5.07 us (5%)
  between operations  1.29 us (1%)
    pallas_call x1, Pallas kernels, per_device(): pl.pallas_call(functools.partial(kernel, row_n, col_n, keep_n, fold), out...  85.8 us
    unnamed x2, local copies, waits for them, and re-layouts  3.83 us

profile of v1, /device:TPU:0, one launch (start us, length us, event | category | flops | bytes accessed | tf_op | source)
XLA Modules:
  0.0 92.2 jit_solution(13900463555278064107)
XLA Ops:
  1.3 85.8 %shard_map.112 = (f32[42,4096]{1,0:T(8,128)}, f32[43,2048]{1,0:T(8,128)}, f32[8,128]{1,0:T(8,128)}) custom-call(f32[32,16384]{1,0:T(8,128)} %u_hbm.1, f32[16,16384]{1,0:T(8,128)} %v_hbm.1, f32[40,128]{1,0:T(8,128)} %bitcast.7, f32[40,128]{1,0:T(8,128)} %bitcast.8, f32[1,2048]{1,0:T(1,128)} %bitcast.9, bf16[64,256,256]{2,1,0:T(8,128)(2,1)} %tiles_hbm.1, ...), custom_call_target="tpu_custom_call" | custom-call | tf_op jit(solution)/shard_map/pallas_call | solution.py:402
  87.1 1.2 %slice.3 = f32[2,2]{1,0:T(2,128)} slice(f32[8,128]{1,0:T(8,128)} %get-tuple-element.8), slice={[0:2], [0:2]} | slice | bytes 32 | tf_op jit(solution)/shard_map/slice | solution.py:471
  88.3 2.1 %copy.15 = f32[42,4096]{1,0:T(8,128)} copy(f32[42,4096]{1,0:T(8,128)} %get-tuple-element.12) | data formatting | bytes 1376256
  90.4 1.8 %copy.16 = f32[43,2048]{1,0:T(8,128)} copy(f32[43,2048]{1,0:T(8,128)} %get-tuple-element.13) | data formatting | bytes 704512

commit v2 on v1

--- a/solution.py
+++ b/solution.py
@@ -43,11 +43,11 @@
 
 
 def kernel(
-    row_n, col_n, keep_n, fold, u_hbm, v_hbm, keep_u_hbm, keep_v_hbm, v_next_hbm, tiles_hbm, rows_hbm, cols_hbm,
+    row_n, col_n, keep_n, u_hbm, v_hbm, keep_u_hbm, keep_v_hbm, v_next_hbm, tiles_hbm, rows_hbm, cols_hbm,
     count_hbm,
     u_out, v_out, bi_out,
-    u_in, v_in, u_code, v_code, u_all, v_all, tiles, keep_u, keep_v, v_first, rows_ref, cols_ref, count_ref,
-    u_rows, v_rows, u_vec, v_vec, gram_v_row, gram_v_col, gram_u_col, gram_u_row,
+    u_in, v_in, u_code, v_code, u_all, v_all, tiles, turned, unit, keep_u, keep_v, v_first, rows_ref, cols_ref, count_ref,
+    u_rows, v_rows, u_vec, v_vec, gram_v_col, gram_v_row, gram_u_col, gram_u_row,
     sum_col, sum_row, sum_all, v_gather, u_gather, u_parts, v_parts, u_recv, v_recv,
     row_pick, col_pick, row_put, col_put, picked, products,
     local_sem, init_u_send, init_u_recv, init_v_send, init_v_recv, send_sem, gram_send, gram_recv,
@@ -62,12 +62,11 @@
         return copy
 
     own_v = load(0, v_hbm, v_in)
-    own_u = load(1, u_hbm, u_in)
     own_keep_v = load(2, keep_v_hbm, keep_v)
     own_keep_u = load(3, keep_u_hbm, keep_u)
     own_next = load(4, v_next_hbm, v_first)
     own_places = [load(5, rows_hbm, rows_ref), load(6, cols_hbm, cols_ref), load(7, count_hbm, count_ref)]
-    own_t = load(8, tiles_hbm, tiles)
+    own_u = load(1, u_hbm, u_in)
 
     barrier = pltpu.get_barrier_semaphore()
     for k in range(1, row_n):
@@ -88,8 +87,12 @@
     slots = tiles.shape[0]
     u_sub, v_sub = u_len // tile, v_len // tile
     row_blocks, col_blocks = col_n * u_sub, row_n * v_sub
-    width = LANE // fold
-    part = rows_p // fold
+    real = keep_n + 1
+    starts, places = [], 0
+    for g in range(-(-real // 8)):
+        starts.append((8 * g, places - 8 * g))
+        places += real - 8 * g
+    assert places <= LANE
 
     def send(axis, me, n, src, dst, sends, recvs):
         copies = []
@@ -106,17 +109,36 @@
         for copy in copies:
             copy.wait()
 
-    u_rows[...] = jnp.zeros(u_rows.shape, F32)
-    v_rows[...] = jnp.zeros(v_rows.shape, F32)
+    sent = []
+
+    def flight(copies, between=lambda: None):
+        for copy in sent:
+            copy.wait_send()
+        sent[:] = copies
+        between()
+        for copy in copies:
+            copy.wait_recv()
+
+    phases = [0]
+
+    def send_sems():
+        turn = phases[0] % 2
+        phases[0] += 1
+        return lambda k: send_sem.at[turn, k]
+
+    blank = keep_n // 8 * 8
+    u_rows[blank:rows_p, :] = jnp.zeros((rows_p - blank, u_len), F32)
+    v_rows[blank:rows_p, :] = jnp.zeros((rows_p - blank, v_len), F32)
     own_v.wait()
     for p in range(row_n):
         v_code[p] = encode(v_in[:, p * v_len:(p + 1) * v_len])
-    own_u.wait()
-    for p in range(col_n):
-        u_code[p] = encode(u_in[:, p * u_len:(p + 1) * u_len])
     pl.semaphore_wait(barrier, row_n + col_n - 2)
     v_init = send("row", row_me, row_n, lambda p: v_code.at[p], lambda k: v_all.at[row_me],
                   lambda k: init_v_send.at[k], lambda k: init_v_recv.at[k])
+    own_u.wait()
+    own_t = load(8, tiles_hbm, tiles)
+    for p in range(col_n):
+        u_code[p] = encode(u_in[:, p * u_len:(p + 1) * u_len])
     u_init = send("col", col_me, col_n, lambda p: u_code.at[p], lambda k: u_all.at[col_me],
                   lambda k: init_u_send.at[k], lambda k: init_u_recv.at[k])
     v_all[row_me] = v_code[row_me]
@@ -138,6 +160,19 @@
     hot_of(rows_ref[...], row_blocks, row_pick, row_put)
     hot_of(cols_ref[...], col_blocks, col_pick, col_put)
 
+    own_t.wait()
+    unit[...] = jnp.where(lax.broadcasted_iota(I32, (tile, tile), 0) == lax.broadcasted_iota(I32, (tile, tile), 1),
+                          1.0, 0.0).astype(BF16)
+
+    def turn(g, carry):
+        base = pl.multiple_of(g * 8, 8)
+        for i in range(8):
+            turned[base + i] = lax.dot_general(unit[...], tiles[base + i], (((1,), (1,)), ((), ())),
+                                               preferred_element_type=F32).astype(BF16)
+        return carry
+
+    lax.fori_loop(0, slots // 8, turn, 0)
+
     row_id = lax.broadcasted_iota(I32, (rows_p, LANE), 0)
     lane_id = lax.broadcasted_iota(I32, (rows_p, LANE), 1)
     lane_row = lax.broadcasted_iota(I32, (1, LANE), 1)
@@ -160,26 +195,26 @@
             buf[pl.ds(me, 1), :] = row
             pairs = [(a, b) for a in range(row_n) for b in range(col_n) if a or b]
             pairs.sort(key=lambda p: -(p[0] // 2 + bin(p[1]).count("1")))
-            copies = []
+            copies, sends = [], send_sems()
             for k, (a, b) in enumerate(pairs):
                 where = {"row": partner(row_me, a, row_n), "col": partner(col_me, b, col_n)}
                 copy = pltpu.make_async_remote_copy(
-                    src_ref=buf.at[pl.ds(me, 1)], dst_ref=buf.at[pl.ds(me, 1)], send_sem=send_sem.at[k],
+                    src_ref=buf.at[pl.ds(me, 1)], dst_ref=buf.at[pl.ds(me, 1)], send_sem=sends(k),
                     recv_sem=sum_all_sem.at[index, k], device_id=where,
                     device_id_type=pl.DeviceIdType.MESH)
                 copy.start()
                 copies.append(copy)
-            finish(copies)
+            flight(copies)
             return jnp.sum(buf[...], axis=0, keepdims=True)
         buf = sum_col.at[index]
         buf[pl.ds(col_me, 1), :] = row
-        finish(send("col", col_me, col_n, lambda p: buf.at[pl.ds(col_me, 1)], lambda k: buf.at[pl.ds(col_me, 1)],
-                    lambda k: send_sem.at[k], lambda k: sum_col_sem.at[index, k]))
+        flight(send("col", col_me, col_n, lambda p: buf.at[pl.ds(col_me, 1)], lambda k: buf.at[pl.ds(col_me, 1)],
+                    send_sems(), lambda k: sum_col_sem.at[index, k]))
         row = jnp.sum(buf[...], axis=0, keepdims=True)
         buf = sum_row.at[index]
         buf[pl.ds(row_me, 1), :] = row
-        finish(send("row", row_me, row_n, lambda p: buf.at[pl.ds(row_me, 1)], lambda k: buf.at[pl.ds(row_me, 1)],
-                    lambda k: send_sem.at[k], lambda k: sum_row_sem.at[index, k]))
+        flight(send("row", row_me, row_n, lambda p: buf.at[pl.ds(row_me, 1)], lambda k: buf.at[pl.ds(row_me, 1)],
+                    send_sems(), lambda k: sum_row_sem.at[index, k]))
         return jnp.sum(buf[...], axis=0, keepdims=True)
 
     def coef(basis, place):
@@ -200,9 +235,7 @@
         got = jnp.where(lane_row < place, row, 0.0)
         square = jnp.sum(jnp.where(lane_row == place, row, 0.0), axis=1, keepdims=True)
         column = jnp.sum(both * got, axis=1, keepdims=True)
-        after = jnp.sum(left * got, axis=1, keepdims=True)
-        first = jnp.sum(one * got, axis=1, keepdims=True)
-        square = square - jnp.sum(column * (first + after), axis=0, keepdims=True)
+        square = square - jnp.sum(column * jnp.sum((one + left) * got, axis=1, keepdims=True), axis=0, keepdims=True)
         scale = jnp.sqrt(square + 1e-06)
         inverse = 1.0 / scale
         spread = jnp.broadcast_to(jnp.where(row_id[:, 0:1] == place, 1.0, -column), (rows_p, LANE))
@@ -217,7 +250,7 @@
                 basis[place:place + 1, s * tile:(s + 1) * tile] = out[s:s + 1, :]
             if gram is None:
                 return None
-            cross = after * inverse
+            cross = jnp.sum(left * got, axis=1, keepdims=True) * inverse
             grown = jnp.where(row_id == place, to_row(cross), gram)
             grown = jnp.where(lane_id == place, cross, grown)
             corner = (row_id == place) & (lane_id == place)
@@ -225,7 +258,7 @@
 
         return scale, out, grow
 
-    def matvec(gathered, n, pick, put, contract):
+    def matvec(gathered, n, pick, put, blocks):
         full = jnp.concatenate([gathered[i].astype(F32) for i in range(n)], axis=0).astype(BF16)
         picked[...] = jnp.dot(pick[...], full, preferred_element_type=F32)
         sub = lax.broadcasted_iota(I32, (8, tile), 0)
@@ -233,8 +266,7 @@
             left = picked[g * 8:(g + 1) * 8, :].astype(BF16)
             acc = jnp.zeros((8, tile), F32)
             for i in range(8):
-                res = lax.dot_general(left, tiles[g * 8 + i], (((1,), (contract,)), ((), ())),
-                                      preferred_element_type=F32)
+                res = jnp.dot(left, blocks[g * 8 + i], preferred_element_type=F32)
                 acc = jnp.where(sub == i, res, acc)
             products[g * 8:(g + 1) * 8, :] = acc
         full = products[...]
@@ -246,14 +278,12 @@
 
     def gather(axis, me, n, own, buf, sems, between):
         buf[me] = own.astype(BF16)
-        copies = send(axis, me, n, lambda p: buf.at[me], lambda k: buf.at[me], lambda k: send_sem.at[k], sems)
-        between()
-        finish(copies)
-
-    def scatter(axis, me, n, value, basis, place, sub, parts, recv, sems):
+        flight(send(axis, me, n, lambda p: buf.at[me], lambda k: buf.at[me], send_sems(), sems), between)
+
+    def scatter(axis, me, n, value, basis, place, sub, parts, recv, sems, between=lambda: None):
         for i in range(n):
             parts[i] = value[i * sub:(i + 1) * sub, :]
-        finish(send(axis, me, n, lambda p: parts.at[p], lambda k: recv.at[k], lambda k: send_sem.at[k], sems))
+        flight(send(axis, me, n, lambda p: parts.at[p], lambda k: recv.at[k], send_sems(), sems), between)
         total = parts[me]
         for k in range(1, n):
             total = total + recv[k]
@@ -279,14 +309,23 @@
         wide = basis[...]
         small = lax.dot_general(wide, wide, (((1,), (1,)), ((), ())), precision=HIGH, preferred_element_type=F32)
         full = jnp.concatenate([small, jnp.zeros((rows_p, LANE - rows_p), F32)], axis=1)
-        packed = full[0:part]
-        for g in range(1, fold):
-            packed = packed + pltpu.roll(full[g * part:(g + 1) * part], g * width, 1)
+        packed = jnp.zeros((8, LANE), F32)
+        for at, shift in starts:
+            block = jnp.where((lane_id[0:8] >= at) & (lane_id[0:8] < real), full[at:at + 8], 0.0)
+            packed = packed + (pltpu.roll(block, shift, 1) if shift else block)
         return packed
 
     def unpack(packed):
-        pieces = [packed] + [pltpu.roll(packed, LANE - g * width, 1) for g in range(1, fold)]
-        return jnp.where(lane_id < width, jnp.concatenate(pieces, axis=0), 0.0)
+        pieces = []
+        for at, shift in starts:
+            block = pltpu.roll(packed, LANE - shift, 1) if shift else packed
+            pieces.append(jnp.where((lane_id[0:8] >= at) & (lane_id[0:8] < real), block, 0.0))
+        pieces.append(jnp.zeros((LANE - 8 * len(pieces), LANE), F32))
+        upper = jnp.concatenate(pieces, axis=0)
+        row_block = lax.div(lax.broadcasted_iota(I32, (LANE, LANE), 0), 8)
+        lane_block = lax.div(lax.broadcasted_iota(I32, (LANE, LANE), 1), 8)
+        full = upper + jnp.transpose(jnp.where(lane_block > row_block, upper, 0.0))
+        return full[0:rows_p]
 
     def row_spread(buf, value, index):
         buf[row_me] = value
@@ -298,27 +337,32 @@
         return send("col", col_me, col_n, lambda p: buf.at[col_me], lambda k: buf.at[col_me],
                     lambda k: gram_send.at[index, k], lambda k: gram_recv.at[index, k])
 
+    early = []
     own_next.wait()
     own_keep_v.wait()
     own_keep_u.wait()
     v_rows[keep_n:keep_n + 1, :] = v_first[...]
     finish(v_init)
     kept(keep_v, v_all, v_rows)
-    v_copies = row_spread(gram_v_row, half_gram(v_rows), 0)
+    v_copies = col_spread(gram_v_col, half_gram(v_rows), 0)
+    finish(v_copies)
+    v_copies = row_spread(gram_v_row, add_up(gram_v_col, col_n), 1)
     finish(u_init)
     kept(keep_u, u_all, u_rows)
-    u_copies = col_spread(gram_u_col, half_gram(u_rows), 1)
+    u_copies = col_spread(gram_u_col, half_gram(u_rows), 2)
     finish(v_copies)
-    v_copies = col_spread(gram_v_col, add_up(gram_v_row, row_n), 2)
-    finish(u_copies)
-    u_copies = row_spread(gram_u_row, add_up(gram_u_col, col_n), 3)
-    finish(v_copies)
-    wide = unpack(add_up(gram_v_col, col_n)) / v_total
+    wide = unpack(add_up(gram_v_row, row_n)) * (1.0 / v_total)
     first_row = wide[keep_n:keep_n + 1, :]
     gram_v = jnp.where((row_id < keep_n) & (lane_id < keep_n), wide, 0.0)
     scale, out, grow = orth(v_rows, v_vec, first_row, keep_n, tables(gram_v, keep_n))
 
     state = {"v": gram_v, "u": None}
+
+    def write_kept():
+        if blank:
+            early.append(load(11, u_rows.at[0:blank], u_out.at[0:blank]))
+            early.append(load(12, v_rows.at[0:blank], v_out.at[0:blank]))
+
 
     def between_v(place, grow, step):
         def run():
@@ -326,10 +370,14 @@
             state["v_table"] = tables(state["v"], place + 1)
             if step == 0:
                 finish(u_copies)
-                gram_u = unpack(add_up(gram_u_row, row_n)) / u_total
-                state["u"] = jnp.where((row_id < keep_n) & (lane_id < keep_n), gram_u, 0.0)
-                state["u_table"] = tables(state["u"], keep_n)
+                u_copies[:] = row_spread(gram_u_row, add_up(gram_u_col, col_n), 3)
         return run
+
+    def gram_end():
+        finish(u_copies)
+        gram_u = unpack(add_up(gram_u_row, row_n)) * (1.0 / u_total)
+        state["u"] = jnp.where((row_id < keep_n) & (lane_id < keep_n), gram_u, 0.0)
+        state["u_table"] = tables(state["u"], keep_n)
 
     def between_u(place, grow, step):
         def run():
@@ -345,19 +393,17 @@
         u_place, v_place = keep_n + step, keep_n + 1 + step
         gather("row", row_me, row_n, out, v_gather.at[step], lambda k: vg_sem.at[step, k],
                between_v(v_place - 1, grow, step))
-        if step == 0:
-            own_t.wait()
-        partial = matvec(v_gather.at[step], row_n, col_pick, row_put, 1)
+        partial = matvec(v_gather.at[step], row_n, col_pick, row_put, turned)
         scatter("col", col_me, col_n, partial, u_rows, u_place, u_sub, u_parts, u_recv.at[step],
-                lambda k: ur_sem.at[step, k])
-        row = sum_all_devices(coef(u_rows, u_place), 2 * step) / u_total
+                lambda k: ur_sem.at[step, k], gram_end if step == 0 else write_kept if step == 1 else lambda: None)
+        row = sum_all_devices(coef(u_rows, u_place), 2 * step) * (1.0 / u_total)
         alpha, out, grow = orth(u_rows, u_vec, row, u_place, state["u_table"])
         gather("col", col_me, col_n, out, u_gather.at[step], lambda k: ug_sem.at[step, k],
                between_u(u_place, grow, step))
-        partial = matvec(u_gather.at[step], col_n, row_pick, col_put, 0)
+        partial = matvec(u_gather.at[step], col_n, row_pick, col_put, tiles)
         scatter("row", row_me, row_n, partial, v_rows, v_place, v_sub, v_parts, v_recv.at[step],
                 lambda k: vr_sem.at[step, k])
-        row = sum_all_devices(coef(v_rows, v_place), 2 * step + 1) / v_total
+        row = sum_all_devices(coef(v_rows, v_place), 2 * step + 1) * (1.0 / v_total)
         beta, out, grow = orth(v_rows, v_vec, row, v_place, state["v_table"])
         alphas.append(alpha)
         betas.append(beta)
@@ -369,8 +415,29 @@
         result = jnp.where((place_r == 0) & (place_l == step), alphas[step], result)
         result = jnp.where((place_r == 1) & (place_l == step), betas[step], result)
     bi_out[...] = result
-    u_out[...] = u_rows[0:u_out.shape[0], :]
-    v_out[...] = v_rows[0:v_out.shape[0], :]
+    copies = [load(9, u_rows.at[blank:rows_p], u_out.at[blank:rows_p]),
+              load(10, v_rows.at[blank:rows_p], v_out.at[blank:rows_p])]
+    for copy in sent:
+        copy.wait_send()
+    finish(early)
+    finish(copies)
+
+
+def close(u_ref, v_ref, bi_ref, u_out, v_out, bi_out, u_in, v_in, bi_in, u_fit, v_fit, bi_fit, sem):
+    sources = ((u_ref, u_in), (v_ref, v_in), (bi_ref, bi_in))
+    loads = [pltpu.make_async_copy(a, b, sem.at[i]) for i, (a, b) in enumerate(sources)]
+    for copy in loads:
+        copy.start()
+    stores = []
+    for i, (copy, (here, fit, there)) in enumerate(zip(
+            loads, ((u_in, u_fit, u_out), (v_in, v_fit, v_out), (bi_in, bi_fit, bi_out)))):
+        copy.wait()
+        fit[...] = here[0:fit.shape[0], 0:fit.shape[1]]
+        store = pltpu.make_async_copy(fit, there, sem.at[3 + i])
+        store.start()
+        stores.append(store)
+    for store in stores:
+        store.wait()
 
 
 def per_device(
@@ -383,8 +450,7 @@
     u_len = u_start.shape[1] // col_n
     v_len = v_start.shape[1] // row_n
     slots, tile = tile_blocks.shape[0], tile_blocks.shape[1]
-    fold = max(f for f in (1, 2, 3) if f * (keep_n + 1) <= LANE)
-    rows_p = -(-(keep_n + 1 + STEPS) // (8 * fold)) * 8 * fold
+    rows_p = -(-(keep_n + 1 + STEPS) // 8) * 8
     keep_p = -(-keep_n // 8) * 8
     assert rows_p <= LANE
     pad = ((0, keep_p - keep_n), (0, 0))
@@ -392,22 +458,21 @@
     total_n = row_n * col_n
     direct_n = total_n if total_n <= DIRECT else 1
     staged = 1 if total_n <= DIRECT else sums
-    part = rows_p // fold
     dma = pltpu.SemaphoreType.DMA
     vmem = pl.BlockSpec(memory_space=pltpu.VMEM)
     hbm = pl.BlockSpec(memory_space=pltpu.HBM)
     u_sub, v_sub = u_len // tile, v_len // tile
     row_blocks, col_blocks = col_n * u_sub, row_n * v_sub
     most = max(row_n, col_n)
-    u_basis, v_basis, bidiagonal = pl.pallas_call(
-        functools.partial(kernel, row_n, col_n, keep_n, fold),
+    padded = pl.pallas_call(
+        functools.partial(kernel, row_n, col_n, keep_n),
         out_shape=(
-            jax.ShapeDtypeStruct((keep_n + STEPS, u_len), F32),
-            jax.ShapeDtypeStruct((keep_n + 1 + STEPS, v_len), F32),
+            jax.ShapeDtypeStruct((rows_p, u_len), F32),
+            jax.ShapeDtypeStruct((rows_p, v_len), F32),
             jax.ShapeDtypeStruct((8, LANE), F32),
         ),
         in_specs=[hbm] * 9,
-        out_specs=(vmem, vmem, vmem),
+        out_specs=(hbm, hbm, vmem),
         scratch_shapes=[
             pltpu.VMEM(u_start.shape, F32),
             pltpu.VMEM(v_start.shape, F32),
@@ -416,6 +481,8 @@
             pltpu.VMEM((col_n, u_here, u_len), I16),
             pltpu.VMEM((row_n, v_here, v_len), I16),
             pltpu.VMEM(tile_blocks.shape, BF16),
+            pltpu.VMEM(tile_blocks.shape, BF16),
+            pltpu.VMEM((tile, tile), BF16),
             pltpu.VMEM((keep_p, basis), F32),
             pltpu.VMEM((keep_p, basis), F32),
             pltpu.VMEM((1, v_len), F32),
@@ -426,10 +493,10 @@
             pltpu.VMEM((rows_p, v_len), F32),
             pltpu.VMEM((u_sub, tile), F32),
             pltpu.VMEM((v_sub, tile), F32),
-            pltpu.VMEM((row_n, part, LANE), F32),
-            pltpu.VMEM((col_n, part, LANE), F32),
-            pltpu.VMEM((col_n, part, LANE), F32),
-            pltpu.VMEM((row_n, part, LANE), F32),
+            pltpu.VMEM((col_n, 8, LANE), F32),
+            pltpu.VMEM((row_n, 8, LANE), F32),
+            pltpu.VMEM((col_n, 8, LANE), F32),
+            pltpu.VMEM((row_n, 8, LANE), F32),
             pltpu.VMEM((staged, col_n, LANE), F32),
             pltpu.VMEM((staged, row_n, LANE), F32),
             pltpu.VMEM((sums, direct_n, LANE), F32),
@@ -445,12 +512,12 @@
             pltpu.VMEM((col_blocks, 3 * slots), BF16),
             pltpu.VMEM((slots, tile), F32),
             pltpu.VMEM((slots, tile), F32),
-            dma((9,)),
+            dma((13,)),
             dma((col_n,)),
             dma((col_n,)),
             dma((row_n,)),
             dma((row_n,)),
-            dma((max(most, direct_n),)),
+            dma((2, max(most, direct_n))),
             dma((4, most)),
             dma((4, most)),
             dma((staged, col_n)),
@@ -468,7 +535,19 @@
         u_start, v_start, jnp.pad(keep_u.T, pad), jnp.pad(keep_v.T, pad), v_next.reshape(1, -1), tile_blocks,
         tile_rows.reshape(1, -1), tile_cols.reshape(1, -1), tile_count.reshape(1, 1),
     )
-    return u_basis, v_basis, bidiagonal[:2, :STEPS]
+    final = (
+        jax.ShapeDtypeStruct((keep_n + STEPS, u_len), F32),
+        jax.ShapeDtypeStruct((keep_n + 1 + STEPS, v_len), F32),
+        jax.ShapeDtypeStruct((2, STEPS), F32),
+    )
+    return pl.pallas_call(
+        close,
+        out_shape=final,
+        in_specs=[hbm] * 3,
+        out_specs=(hbm, hbm, hbm),
+        scratch_shapes=[pltpu.VMEM(x.shape, F32) for x in (*padded, *final)] + [dma((6,))],
+        compiler_params=pltpu.CompilerParams(vmem_limit_bytes=62 * 1024 * 1024),
+    )(*padded)
 
 
 def solution(mesh):

time: 92.4 us -> 87.6 us (0.948)
  local copies, waits for them, and re-layouts: 5.07 us -> 0 us
    unnamed x2 -> x0, local copies, waits for them, and re-layouts: 3.83 us -> none
    slice x1 -> x0, local copies, waits for them, and re-layouts: 1.24 us -> none  [per_device(): return (u_basis, v_basis, bidiagonal[:2, :STEPS])]
    pallas_call x1 -> x2, Pallas kernels: 85.8 us -> 86.2 us  [the longest x1 83.9 us: per_device(): pl.pallas_call(functools.partial(kernel, row_n, col_n, keep_n), out_shape...]
where the time goes in v2:
time: 87.6 us; the launch traced here: 87.5 us
  Pallas kernels  86.2 us (98%)
  between operations  1.29 us (1%)
    pallas_call x1, Pallas kernels, per_device(): pl.pallas_call(functools.partial(kernel, row_n, col_n, keep_n), out_shape...  83.9 us
    pallas_call x1, Pallas kernels, per_device(): pl.pallas_call(close, out_shape=final, in_specs=[hbm] * 3, out_specs=(hbm...  2.25 us

profile of v2, /device:TPU:0, one launch (start us, length us, event | category | flops | bytes accessed | tf_op | source)
XLA Modules:
  0.0 87.5 jit_solution(17632192004542545076)
XLA Ops:
  1.3 83.9 %shard_map.112 = (f32[48,4096]{1,0:T(8,128)}, f32[48,2048]{1,0:T(8,128)}, f32[8,128]{1,0:T(8,128)}) custom-call(f32[32,16384]{1,0:T(8,128)} %u_hbm.1, f32[16,16384]{1,0:T(8,128)} %v_hbm.1, f32[40,128]{1,0:T(8,128)} %bitcast.7, f32[40,128]{1,0:T(8,128)} %bitcast.8, f32[1,2048]{1,0:T(1,128)} %bitcast.9, bf16[64,256,256]{2,1,0:T(8,128)(2,1)} %tiles_hbm.1, ...), custom_call_target="tpu_custom_call" | custom-call | tf_op jit(solution)/shard_map/pallas_call | solution.py:467
  85.2 2.2 %shard_map.113 = (f32[42,4096]{1,0:T(8,128)}, f32[43,2048]{1,0:T(8,128)}, f32[2,2]{1,0:T(2,128)}) custom-call(f32[48,4096]{1,0:T(8,128)} %get-tuple-element.6.u_ref, f32[48,2048]{1,0:T(8,128)} %get-tuple-element.7.v_ref, f32[8,128]{1,0:T(8,128)} %get-tuple-element.8.bi_ref), custom_call_target="tpu_custom_call" | custom-call | tf_op jit(solution)/shard_map/pallas_call | solution.py:543

commit v3 on v2

--- a/solution.py
+++ b/solution.py
@@ -18,17 +18,18 @@
 KNEE = 5.0
 FINE = 4800.0
 COARSE = 461.0
-
-
-def encode(x):
-    code = x * COARSE + jnp.clip(x, -KNEE, KNEE) * (FINE - COARSE)
+LARGEST = 24.0
+
+
+def encode(x, coarse=COARSE):
+    code = x * coarse + jnp.clip(x, -KNEE, KNEE) * (FINE - coarse)
     return jnp.round(code).astype(I32).astype(I16)
 
 
-def decode(code):
+def decode(code, coarse=COARSE):
     y = code.astype(I32).astype(F32)
     near = jnp.clip(y, -KNEE * FINE, KNEE * FINE)
-    return near * (1.0 / FINE) + (y - near) * (1.0 / COARSE)
+    return near * (1.0 / FINE) + (y - near) * (1.0 / coarse)
 
 
 def partner(me, k, n):
@@ -49,9 +50,10 @@
     u_in, v_in, u_code, v_code, u_all, v_all, tiles, turned, unit, keep_u, keep_v, v_first, rows_ref, cols_ref, count_ref,
     u_rows, v_rows, u_vec, v_vec, gram_v_col, gram_v_row, gram_u_col, gram_u_row,
     sum_col, sum_row, sum_all, v_gather, u_gather, u_parts, v_parts, u_recv, v_recv,
-    row_pick, col_pick, row_put, col_put, picked, products,
+    row_pick, col_pick, row_put, col_put, picked, products, full_code, full_u, full_y, x_full, new_full,
     local_sem, init_u_send, init_u_recv, init_v_send, init_v_recv, send_sem, gram_send, gram_recv,
     sum_col_sem, sum_row_sem, sum_all_sem, vg_sem, ug_sem, ur_sem, vr_sem,
+    full_send, full_recv, xf_send, xf_recv,
 ):
     row_me = lax.axis_index("row")
     col_me = lax.axis_index("col")
@@ -87,6 +89,7 @@
     slots = tiles.shape[0]
     u_sub, v_sub = u_len // tile, v_len // tile
     row_blocks, col_blocks = col_n * u_sub, row_n * v_sub
+    wide_coarse = (32700.0 - KNEE * FINE) / (LARGEST * keep_u.shape[1] ** 0.5 - KNEE)
     real = keep_n + 1
     starts, places = [], 0
     for g in range(-(-real // 8)):
@@ -188,7 +191,7 @@
                      for i in range(0, len(parts), 2)]
         return parts[0]
 
-    def sum_all_devices(row, index):
+    def sum_all_devices(row, index, between=lambda: None):
         if direct:
             me = row_me * col_n + col_me
             buf = sum_all.at[index]
@@ -204,12 +207,12 @@
                     device_id_type=pl.DeviceIdType.MESH)
                 copy.start()
                 copies.append(copy)
-            flight(copies)
+            flight(copies, between)
             return jnp.sum(buf[...], axis=0, keepdims=True)
         buf = sum_col.at[index]
         buf[pl.ds(col_me, 1), :] = row
         flight(send("col", col_me, col_n, lambda p: buf.at[pl.ds(col_me, 1)], lambda k: buf.at[pl.ds(col_me, 1)],
-                    send_sems(), lambda k: sum_col_sem.at[index, k]))
+                    send_sems(), lambda k: sum_col_sem.at[index, k]), between)
         row = jnp.sum(buf[...], axis=0, keepdims=True)
         buf = sum_row.at[index]
         buf[pl.ds(row_me, 1), :] = row
@@ -230,36 +233,54 @@
         one = jnp.where(eye & (row_id < place), 1.0, 0.0)
         return 2.0 * one - gram, one - (2.0 * gram - square), one
 
-    def orth(basis, vec, row, place, table):
+    def solve(row, place, table):
         both, left, one = table
         got = jnp.where(lane_row < place, row, 0.0)
         square = jnp.sum(jnp.where(lane_row == place, row, 0.0), axis=1, keepdims=True)
         column = jnp.sum(both * got, axis=1, keepdims=True)
         square = square - jnp.sum(column * jnp.sum((one + left) * got, axis=1, keepdims=True), axis=0, keepdims=True)
         scale = jnp.sqrt(square + 1e-06)
-        inverse = 1.0 / scale
+        return got, left, square, column, scale, 1.0 / scale
+
+    def apply(basis, vec, place, found):
+        column, inverse = found[3], found[5]
         spread = jnp.broadcast_to(jnp.where(row_id[:, 0:1] == place, 1.0, -column), (rows_p, LANE))
         for j in range(basis.shape[1] // LANE):
             at = slice(j * LANE, (j + 1) * LANE)
             s, h = j * LANE // tile, j * LANE % tile
             vec[s:s + 1, h:h + LANE] = jnp.sum(spread * basis[:, at], axis=0, keepdims=True)
-        out = vec[...] * inverse
-
-        def grow(gram):
-            for s in range(vec.shape[0]):
-                basis[place:place + 1, s * tile:(s + 1) * tile] = out[s:s + 1, :]
-            if gram is None:
-                return None
-            cross = jnp.sum(left * got, axis=1, keepdims=True) * inverse
-            grown = jnp.where(row_id == place, to_row(cross), gram)
-            grown = jnp.where(lane_id == place, cross, grown)
-            corner = (row_id == place) & (lane_id == place)
-            return jnp.where(corner, square / (scale * scale), grown)
-
-        return scale, out, grow
-
-    def matvec(gathered, n, pick, put, blocks):
-        full = jnp.concatenate([gathered[i].astype(F32) for i in range(n)], axis=0).astype(BF16)
+        return vec[...] * inverse
+
+    def grow_basis(basis, place, found, out, gram):
+        got, left, square, column, scale, inverse = found
+        for s in range(out.shape[0]):
+            basis[place:place + 1, s * tile:(s + 1) * tile] = out[s:s + 1, :]
+        if gram is None:
+            return None
+        cross = jnp.sum(left * got, axis=1, keepdims=True) * inverse
+        grown = jnp.where(row_id == place, to_row(cross), gram)
+        grown = jnp.where(lane_id == place, cross, grown)
+        corner = (row_id == place) & (lane_id == place)
+        return jnp.where(corner, square / (scale * scale), grown)
+
+    def apply_full(step, found):
+        column, inverse = found[3], found[5]
+        spread = jnp.broadcast_to(jnp.where(row_id[0:keep_p, 0:1] < keep_n, -column[0:keep_p], 0.0), (keep_p, LANE))
+        for q in range(col_n):
+            for j in range(u_len // LANE):
+                at = slice(j * LANE, (j + 1) * LANE)
+                s, h = q * u_sub + j * LANE // tile, j * LANE % tile
+                full_y[s:s + 1, h:h + LANE] = jnp.sum(spread * full_u[q, :, at], axis=0, keepdims=True)
+        x = jnp.concatenate([x_full[step, q] for q in range(col_n)], axis=0)
+        for old in range(step):
+            before = jnp.concatenate([new_full[old, q] for q in range(col_n)], axis=0)
+            x = x - column[keep_n + old:keep_n + old + 1, 0:1] * before
+        return (x + full_y[...]) * inverse
+
+    def joined(gathered, n):
+        return jnp.concatenate([gathered[i].astype(F32) for i in range(n)], axis=0).astype(BF16)
+
+    def matvec(full, pick, put, blocks):
         picked[...] = jnp.dot(pick[...], full, preferred_element_type=F32)
         sub = lax.broadcasted_iota(I32, (8, tile), 0)
         for g in range(slots // 8):
@@ -289,6 +310,7 @@
             total = total + recv[k]
         for s in range(sub):
             basis[place:place + 1, s * tile:(s + 1) * tile] = total[s:s + 1, :]
+        return total
 
     def kept(keep, source, target):
         factor = keep[...]
@@ -345,16 +367,29 @@
     finish(v_init)
     kept(keep_v, v_all, v_rows)
     v_copies = col_spread(gram_v_col, half_gram(v_rows), 0)
-    finish(v_copies)
-    v_copies = row_spread(gram_v_row, add_up(gram_v_col, col_n), 1)
     finish(u_init)
     kept(keep_u, u_all, u_rows)
     u_copies = col_spread(gram_u_col, half_gram(u_rows), 2)
+    full_copies = []
+    cut = u_len * 3 // 4
+
+    def full_spread(index, a, b):
+        full_copies.extend(send(
+            "col", col_me, col_n, lambda p: full_code.at[col_me, :, a:b], lambda k: full_code.at[col_me, :, a:b],
+            lambda k: full_send.at[index, k], lambda k: full_recv.at[index, k]))
+
+    full_code[col_me] = encode(u_rows[0:keep_p, :], wide_coarse)
+    full_spread(0, 0, cut)
+    finish(v_copies)
+    v_copies = row_spread(gram_v_row, add_up(gram_v_col, col_n), 1)
+    finish(u_copies)
+    u_copies = row_spread(gram_u_row, add_up(gram_u_col, col_n), 3)
     finish(v_copies)
     wide = unpack(add_up(gram_v_row, row_n)) * (1.0 / v_total)
     first_row = wide[keep_n:keep_n + 1, :]
     gram_v = jnp.where((row_id < keep_n) & (lane_id < keep_n), wide, 0.0)
-    scale, out, grow = orth(v_rows, v_vec, first_row, keep_n, tables(gram_v, keep_n))
+    found = solve(first_row, keep_n, tables(gram_v, keep_n))
+    out = apply(v_rows, v_vec, keep_n, found)
 
     state = {"v": gram_v, "u": None}
 
@@ -364,14 +399,23 @@
             early.append(load(12, v_rows.at[0:blank], v_out.at[0:blank]))
 
 
-    def between_v(place, grow, step):
+    def between_v(place, found, out, step):
         def run():
-            state["v"] = grow(state["v"])
+            state["v"] = grow_basis(v_rows, place, found, out, state["v"])
             state["v_table"] = tables(state["v"], place + 1)
-            if step == 0:
-                finish(u_copies)
-                u_copies[:] = row_spread(gram_u_row, add_up(gram_u_col, col_n), 3)
+            if step == 1:
+                finish(full_copies)
+                for q in range(col_n):
+                    full_u[q] = decode(full_code[q], wide_coarse)
+                full_u[col_me] = u_rows[0:keep_p, :]
         return run
+
+    def grow_u(place, found, out, step):
+        if step + 1 < STEPS:
+            state["u"] = grow_basis(u_rows, place, found, out, state["u"])
+            state["u_table"] = tables(state["u"], place + 1)
+        else:
+            grow_basis(u_rows, place, found, out, None)
 
     def gram_end():
         finish(u_copies)
@@ -388,26 +432,63 @@
                 grow(None)
         return run
 
+    def between_u(place, found, out, step):
+        return lambda: grow_u(place, found, out, step)
+
+    def share_new(out):
+        def run():
+            full_spread(1, cut, u_len)
+            new_full[0, col_me] = out
+            full_copies.extend(send(
+                "col", col_me, col_n, lambda p: new_full.at[0, col_me], lambda k: new_full.at[0, col_me],
+                lambda k: xf_send.at[0, k], lambda k: xf_recv.at[0, k]))
+        return run
+
+    def late_u(place, found, step):
+        return lambda: grow_u(place, found, apply(u_rows, u_vec, place, found), step)
+
     alphas, betas = [], []
     for step in range(STEPS):
         u_place, v_place = keep_n + step, keep_n + 1 + step
         gather("row", row_me, row_n, out, v_gather.at[step], lambda k: vg_sem.at[step, k],
-               between_v(v_place - 1, grow, step))
-        partial = matvec(v_gather.at[step], row_n, col_pick, row_put, turned)
-        scatter("col", col_me, col_n, partial, u_rows, u_place, u_sub, u_parts, u_recv.at[step],
-                lambda k: ur_sem.at[step, k], gram_end if step == 0 else write_kept if step == 1 else lambda: None)
-        row = sum_all_devices(coef(u_rows, u_place), 2 * step) * (1.0 / u_total)
-        alpha, out, grow = orth(u_rows, u_vec, row, u_place, state["u_table"])
-        gather("col", col_me, col_n, out, u_gather.at[step], lambda k: ug_sem.at[step, k],
-               between_u(u_place, grow, step))
-        partial = matvec(u_gather.at[step], col_n, row_pick, col_put, tiles)
+               between_v(v_place - 1, found, out, step))
+        partial = matvec(joined(v_gather.at[step], row_n), col_pick, row_put, turned)
+        total = scatter("col", col_me, col_n, partial, u_rows, u_place, u_sub, u_parts, u_recv.at[step],
+                        lambda k: ur_sem.at[step, k],
+                        gram_end if step == 0 else write_kept if step == 1 else lambda: None)
+        if step == 0:
+            row = sum_all_devices(coef(u_rows, u_place), 2 * step) * (1.0 / u_total)
+            found = solve(row, u_place, state["u_table"])
+            out = apply(u_rows, u_vec, u_place, found)
+            gather("col", col_me, col_n, out, u_gather.at[step], lambda k: ug_sem.at[step, k],
+                   between_u(u_place, found, out, step))
+            full, between = joined(u_gather.at[step], col_n), share_new(out) if STEPS > 1 else lambda: None
+        else:
+            x_copies = []
+
+            def share_x(step=step, total=total):
+                x_full[step, col_me] = total
+                x_copies.extend(send(
+                    "col", col_me, col_n, lambda p: x_full.at[step, col_me], lambda k: x_full.at[step, col_me],
+                    lambda k: xf_send.at[step, k], lambda k: xf_recv.at[step, k]))
+
+            row = sum_all_devices(coef(u_rows, u_place), 2 * step, share_x) * (1.0 / u_total)
+            found = solve(row, u_place, state["u_table"])
+            finish(x_copies)
+            wide = apply_full(step, found)
+            if step + 1 < STEPS:
+                for q in range(col_n):
+                    new_full[step, q] = wide[q * u_sub:(q + 1) * u_sub]
+            full, between = wide.astype(BF16), late_u(u_place, found, step)
+        alphas.append(found[4])
+        partial = matvec(full, row_pick, col_put, tiles)
         scatter("row", row_me, row_n, partial, v_rows, v_place, v_sub, v_parts, v_recv.at[step],
-                lambda k: vr_sem.at[step, k])
+                lambda k: vr_sem.at[step, k], between)
         row = sum_all_devices(coef(v_rows, v_place), 2 * step + 1) * (1.0 / v_total)
-        beta, out, grow = orth(v_rows, v_vec, row, v_place, state["v_table"])
-        alphas.append(alpha)
-        betas.append(beta)
-    grow(None)
+        found = solve(row, v_place, state["v_table"])
+        out = apply(v_rows, v_vec, v_place, found)
+        betas.append(found[4])
+    grow_basis(v_rows, keep_n + STEPS, found, out, None)
     place_r = lax.broadcasted_iota(I32, (8, LANE), 0)
     place_l = lax.broadcasted_iota(I32, (8, LANE), 1)
     result = jnp.zeros((8, LANE), F32)
@@ -424,16 +505,24 @@
 
 
 def close(u_ref, v_ref, bi_ref, u_out, v_out, bi_out, u_in, v_in, bi_in, u_fit, v_fit, bi_fit, sem):
-    sources = ((u_ref, u_in), (v_ref, v_in), (bi_ref, bi_in))
-    loads = [pltpu.make_async_copy(a, b, sem.at[i]) for i, (a, b) in enumerate(sources)]
-    for copy in loads:
-        copy.start()
+    pieces = [(bi_ref, bi_in, bi_fit, bi_out, None)]
+    for here, inside, fit, there, n in ((u_ref, u_in, u_fit, u_out, 4), (v_ref, v_in, v_fit, v_out, 2)):
+        step = here.shape[1] // n
+        pieces += [(here, inside, fit, there, slice(i * step, (i + 1) * step)) for i in range(n)]
+    loads = []
+    for i, (here, inside, fit, there, at) in enumerate(pieces):
+        source, target = (here, inside) if at is None else (here.at[:, at], inside.at[:, at])
+        loads.append(pltpu.make_async_copy(source, target, sem.at[0, i]))
+        loads[-1].start()
     stores = []
-    for i, (copy, (here, fit, there)) in enumerate(zip(
-            loads, ((u_in, u_fit, u_out), (v_in, v_fit, v_out), (bi_in, bi_fit, bi_out)))):
-        copy.wait()
-        fit[...] = here[0:fit.shape[0], 0:fit.shape[1]]
-        store = pltpu.make_async_copy(fit, there, sem.at[3 + i])
+    for i, (here, inside, fit, there, at) in enumerate(pieces):
+        loads[i].wait()
+        if at is None:
+            fit[...] = inside[0:fit.shape[0], 0:fit.shape[1]]
+            store = pltpu.make_async_copy(fit, there, sem.at[1, i])
+        else:
+            fit[:, at] = inside[0:fit.shape[0], at]
+            store = pltpu.make_async_copy(fit.at[:, at], there.at[:, at], sem.at[1, i])
         store.start()
         stores.append(store)
     for store in stores:
@@ -512,6 +601,11 @@
             pltpu.VMEM((col_blocks, 3 * slots), BF16),
             pltpu.VMEM((slots, tile), F32),
             pltpu.VMEM((slots, tile), F32),
+            pltpu.VMEM((col_n, keep_p, u_len), I16),
+            pltpu.VMEM((col_n, keep_p, u_len), F32),
+            pltpu.VMEM((row_blocks, tile), F32),
+            pltpu.VMEM((STEPS, col_n, u_sub, tile), F32),
+            pltpu.VMEM((STEPS, col_n, u_sub, tile), F32),
             dma((13,)),
             dma((col_n,)),
             dma((col_n,)),
@@ -527,6 +621,10 @@
             dma((STEPS, col_n)),
             dma((STEPS, col_n)),
             dma((STEPS, row_n)),
+            dma((2, col_n)),
+            dma((2, col_n)),
+            dma((STEPS, col_n)),
+            dma((STEPS, col_n)),
         ],
         compiler_params=pltpu.CompilerParams(
             collective_id=0, has_side_effects=True, vmem_limit_bytes=62 * 1024 * 1024
@@ -545,7 +643,7 @@
         out_shape=final,
         in_specs=[hbm] * 3,
         out_specs=(hbm, hbm, hbm),
-        scratch_shapes=[pltpu.VMEM(x.shape, F32) for x in (*padded, *final)] + [dma((6,))],
+        scratch_shapes=[pltpu.VMEM(x.shape, F32) for x in (*padded, *final)] + [dma((2, 7))],
         compiler_params=pltpu.CompilerParams(vmem_limit_bytes=62 * 1024 * 1024),
     )(*padded)
 

time: 87.6 us -> 86.1 us (0.983)
  Pallas kernels: 86.2 us -> 84.6 us
    pallas_call x1, Pallas kernels: 83.9 us -> 82.5 us  [per_device(): pl.pallas_call(functools.partial(kernel, row_n, col_n, keep_n), out_shape...]
where the time goes in v3:
time: 86.1 us; the launch traced here: 85.9 us
  Pallas kernels  84.6 us (98%)
  between operations  1.29 us (1%)
    pallas_call x1, Pallas kernels, per_device(): pl.pallas_call(functools.partial(kernel, row_n, col_n, keep_n), out_shape...  82.5 us
    pallas_call x1, Pallas kernels, per_device(): pl.pallas_call(close, out_shape=final, in_specs=[hbm] * 3, out_specs=(hbm...  2.17 us

profile of v3, /device:TPU:0, one launch (start us, length us, event | category | flops | bytes accessed | tf_op | source)
XLA Modules:
  0.0 85.9 jit_solution(12459606408592810836)
XLA Ops:
  1.3 82.5 %shard_map.112 = (f32[48,4096]{1,0:T(8,128)}, f32[48,2048]{1,0:T(8,128)}, f32[8,128]{1,0:T(8,128)}) custom-call(f32[32,16384]{1,0:T(8,128)} %u_hbm.1, f32[16,16384]{1,0:T(8,128)} %v_hbm.1, f32[40,128]{1,0:T(8,128)} %bitcast.7, f32[40,128]{1,0:T(8,128)} %bitcast.8, f32[1,2048]{1,0:T(1,128)} %bitcast.9, bf16[64,256,256]{2,1,0:T(8,128)(2,1)} %tiles_hbm.1, ...), custom_call_target="tpu_custom_call" | custom-call | tf_op jit(solution)/shard_map/pallas_call | solution.py:556
  83.8 2.2 %shard_map.113 = (f32[42,4096]{1,0:T(8,128)}, f32[43,2048]{1,0:T(8,128)}, f32[2,2]{1,0:T(2,128)}) custom-call(f32[48,4096]{1,0:T(8,128)} %get-tuple-element.6.u_ref, f32[48,2048]{1,0:T(8,128)} %get-tuple-element.7.v_ref, f32[8,128]{1,0:T(8,128)} %get-tuple-element.8.bi_ref), custom_call_target="tpu_custom_call" | custom-call | tf_op jit(solution)/shard_map/pallas_call | solution.py:641

commit v4 on v3

--- a/solution.py
+++ b/solution.py
@@ -114,11 +114,14 @@
 
     sent = []
 
-    def flight(copies, between=lambda: None):
+    def flight(copies, between=lambda: None, arrived=None):
         for copy in sent:
             copy.wait_send()
         sent[:] = copies
         between()
+        if arrived is not None:
+            arrived.wait()
+            return
         for copy in copies:
             copy.wait_recv()
 
@@ -203,11 +206,12 @@
                 where = {"row": partner(row_me, a, row_n), "col": partner(col_me, b, col_n)}
                 copy = pltpu.make_async_remote_copy(
                     src_ref=buf.at[pl.ds(me, 1)], dst_ref=buf.at[pl.ds(me, 1)], send_sem=sends(k),
-                    recv_sem=sum_all_sem.at[index, k], device_id=where,
+                    recv_sem=sum_all_sem.at[index, 0], device_id=where,
                     device_id_type=pl.DeviceIdType.MESH)
                 copy.start()
                 copies.append(copy)
-            flight(copies, between)
+            rest = buf.at[pl.ds(0, row_n * col_n - 1)]
+            flight(copies, between, pltpu.make_async_copy(rest, rest, sum_all_sem.at[index, 0]))
             return jnp.sum(buf[...], axis=0, keepdims=True)
         buf = sum_col.at[index]
         buf[pl.ds(col_me, 1), :] = row

time: 86.1 us -> 85.9 us (level)
  no operation moved by 1% of the time
where the time goes in v4:
time: 85.9 us; the launch traced here: 85.7 us
  Pallas kernels  84.4 us (98%)
  between operations  1.29 us (2%)
    pallas_call x1, Pallas kernels, per_device(): pl.pallas_call(functools.partial(kernel, row_n, col_n, keep_n), out_shape...  82.3 us
    pallas_call x1, Pallas kernels, per_device(): pl.pallas_call(close, out_shape=final, in_specs=[hbm] * 3, out_specs=(hbm...  2.17 us

profile of v4, /device:TPU:0, one launch (start us, length us, event | category | flops | bytes accessed | tf_op | source)
XLA Modules:
  0.0 85.7 jit_solution(6613518278440171413)
XLA Ops:
  1.3 82.3 %shard_map.112 = (f32[48,4096]{1,0:T(8,128)}, f32[48,2048]{1,0:T(8,128)}, f32[8,128]{1,0:T(8,128)}) custom-call(f32[32,16384]{1,0:T(8,128)} %u_hbm.1, f32[16,16384]{1,0:T(8,128)} %v_hbm.1, f32[40,128]{1,0:T(8,128)} %bitcast.7, f32[40,128]{1,0:T(8,128)} %bitcast.8, f32[1,2048]{1,0:T(1,128)} %bitcast.9, bf16[64,256,256]{2,1,0:T(8,128)(2,1)} %tiles_hbm.1, ...), custom_call_target="tpu_custom_call" | custom-call | tf_op jit(solution)/shard_map/pallas_call | solution.py:560
  83.6 2.2 %shard_map.113 = (f32[42,4096]{1,0:T(8,128)}, f32[43,2048]{1,0:T(8,128)}, f32[2,2]{1,0:T(2,128)}) custom-call(f32[48,4096]{1,0:T(8,128)} %get-tuple-element.6.u_ref, f32[48,2048]{1,0:T(8,128)} %get-tuple-element.7.v_ref, f32[8,128]{1,0:T(8,128)} %get-tuple-element.8.bi_ref), custom_call_target="tpu_custom_call" | custom-call | tf_op jit(solution)/shard_map/pallas_call | solution.py:645
